TPU v7x, 32 devices: a whole 2x2x4 slice. The times are simulated.
32 devices in a mesh: seq: 8 (over z, y), head: 4 (over x, core).
Axes of the slice: x: 2, y: 2, z: 4, core: 2. Of those that a mesh axis runs over, the one named last changes fastest.
Arguments:
- query_rows: bfloat16 [8192, 4096], P('seq', 'head'), may hold values from -6 to 6
- key_rows: bfloat16 [8192, 1024], P('seq', 'head'), may hold values from -6 to 6
- value_rows: bfloat16 [8192, 1024], P('seq', 'head'), may hold values from -6 to 6
- attn_out: bfloat16 [8192, 4096], P('seq', 'head'), may hold values from -4 to 4
- out_grad: bfloat16 [8192, 4096], P(('seq', 'head')), may hold values from -6 to 6
- block_index: int32 [64, 8], P('seq'), may hold values from 0 to 63, as said below
- block_count: int32 [64], P('seq'), may hold values from 1 to 8
Outputs:
- query_grad: bfloat16 [8192, 4096], P('seq', 'head')
- key_grad: bfloat16 [8192, 1024], P('seq', 'head')
- value_grad: bfloat16 [8192, 1024], P('seq', 'head')
Inputs may be any that keep to these rules, and one draw needn't show every extreme that they name: `block_index`: row i lists distinct blocks, all at or before block i; its first entry is block i, and blocks i - 1, i - 2 and 0 are listed wherever they exist and differ from i. Entries at or past block_count[i] repeat block i. Counting with repetition the entries of the 8 query blocks of one index of seq that name blocks held by another index, leaving out block 0 and, for the index just below, its last two blocks: at most 4 for any pair of indices, and exactly 4 for some pair in every draw.
All inputs are finite; a program needn't handle non-finite values.
Results may differ from a plain program's by a relative error of at most 0.006.
Values may be sent and summed in bfloat16 or wider, within the bound.
A program may use at most 128 MiB of HBM per device.

v0:
```python
import jax
import jax.numpy as jnp
from jax import lax
from jax.sharding import PartitionSpec as P

HD = 128
GROUP = 4
BLK = 128
NF = 4


def shifted(value, axis, steps):
    count = lax.axis_size(axis)
    initial, last = (max(0, -steps), min(count, count - steps))
    return lax.ppermute(value, axis, [(source, source + steps) for source in range(initial, last)])


def broadcast(x, axis, root):
    mine = lax.axis_index(axis) == root
    return lax.psum(jnp.where(mine, x, jnp.zeros_like(x)), axis)


def plan_blocks(block_index, block_count, device, qblocks, seq_count, capacity):
    owner_dev = block_index // qblocks
    within = block_index % qblocks
    max_blocks = block_index.shape[1]
    is_live = jnp.arange(max_blocks, dtype=jnp.int32)[None, :] < block_count[:, None]
    is_local = owner_dev == device
    is_prev = (owner_dev == device - 1) & (within >= qblocks - 2)
    is_first = (block_index == 0) & jnp.logical_not(is_local) & jnp.logical_not(is_prev)
    is_far = (
        is_live & jnp.logical_not(is_local) & jnp.logical_not(is_prev) & jnp.logical_not(is_first)
    )
    flat_far = is_far.reshape(-1)
    flat_owner = owner_dev.reshape(-1)
    entries = flat_far.shape[0]
    entry_order = jnp.arange(entries, dtype=jnp.int32)
    earlier = (
        flat_far[None, :]
        & (flat_owner[None, :] == flat_owner[:, None])
        & (entry_order[None, :] < entry_order[:, None])
    )
    far_rank = jnp.sum(earlier.astype(jnp.int32), axis=1)
    far_slot = flat_owner * capacity + far_rank
    target_slot = jnp.where(flat_far, far_slot, seq_count * capacity)
    request = (
        jnp.zeros((seq_count * capacity + 1,), jnp.int32).at[target_slot].set(within.reshape(-1))
    )
    request = request[: seq_count * capacity].reshape(seq_count, capacity)
    far_position = qblocks + 3 + far_slot.reshape(block_index.shape)
    position = jnp.where(
        is_local,
        within,
        jnp.where(
            is_prev,
            qblocks + within - (qblocks - 2),
            jnp.where(is_first, qblocks + 2, far_position),
        ),
    )
    remote = (is_far | is_first & is_live).astype(jnp.int32)
    return (position, request, remote)


def local(query_rows, key_rows, value_rows, attn_out, out_grad, block_index, block_count):
    seq_count = lax.axis_size("seq")
    my_index = lax.axis_index("seq")
    grad_rows = lax.all_to_all(out_grad, "head", split_axis=1, concat_axis=0, tiled=True)
    qblocks = query_rows.shape[0] // BLK
    kv_heads = key_rows.shape[1] // HD
    max_blocks = block_index.shape[1]
    capacity = qblocks * NF // seq_count
    kv_width = 2 * kv_heads * HD
    kv_local = jnp.concatenate([key_rows, value_rows], axis=1).reshape(qblocks, BLK, kv_width)
    position, request, remote = plan_blocks(
        block_index, block_count, my_index, qblocks, seq_count, capacity
    )
    asked_rows = lax.all_to_all(request, "seq", split_axis=0, concat_axis=0, tiled=True)
    served = kv_local[asked_rows]
    fetched = lax.all_to_all(served, "seq", split_axis=0, concat_axis=0, tiled=True)
    prev_rows = shifted(kv_local[qblocks - 2 :], "seq", 1)
    first_rows = broadcast(kv_local[0:1], "seq", 0)
    kv_all = jnp.concatenate(
        [kv_local, prev_rows, first_rows, fetched.reshape(seq_count * capacity, BLK, kv_width)],
        axis=0,
    )
    slot_count = kv_all.shape[0]
    query_blocks = query_rows.reshape(qblocks, BLK, kv_heads, GROUP, HD)
    grad_blocks = grad_rows.reshape(qblocks, BLK, kv_heads, GROUP, HD)
    out_blocks = attn_out.reshape(qblocks, BLK, kv_heads, GROUP, HD)
    scale_factor = HD ** (-0.5)
    offsets = jnp.arange(BLK, dtype=jnp.int32)
    half_width = kv_width // 2

    def fetch_tiles(tile_position):
        gathered = kv_all[tile_position]
        count = tile_position.shape[0]
        key_tile = gathered[..., :half_width].reshape(count, BLK, kv_heads, HD)
        value_tile = gathered[..., half_width:].reshape(count, BLK, kv_heads, HD)
        return (key_tile, value_tile)

    def masked_scores(query_tile, key_tile, row_number, tile_index, live):
        scores = (
            jnp.einsum("rgqd,mcgd->gqrmc", query_tile, key_tile, preferred_element_type=jnp.float32)
            * scale_factor
        )
        query_pos = (my_index * qblocks + row_number) * BLK + offsets
        key_pos = tile_index[:, None] * BLK + offsets[None, :]
        allowed = live[:, None][None] & (key_pos[None] <= query_pos[:, None, None])
        return jnp.where(allowed, scores, -jnp.inf)

    def stats_of(masked):
        row_top = jnp.max(masked, axis=(3, 4), keepdims=True)
        row_total = jnp.sum(jnp.exp(masked - row_top), axis=(3, 4), keepdims=True)
        return (row_top, row_total)

    def terms_from(
        masked, row_top, row_total, query_tile, grad_tile, out_tile, key_tile, value_tile
    ):
        count = key_tile.shape[0]
        probs_full = jnp.exp(masked - row_top) / row_total
        probs_low = probs_full.astype(jnp.bfloat16)
        dprobs = jnp.einsum(
            "rgqd,mcgd->gqrmc", grad_tile, value_tile, preferred_element_type=jnp.float32
        )
        out_dot = jnp.sum(grad_tile.astype(jnp.float32) * out_tile.astype(jnp.float32), axis=-1)
        out_dot = jnp.transpose(out_dot, (1, 2, 0))[..., None, None]
        dscores_low = (probs_full * (dprobs - out_dot)).astype(jnp.bfloat16)
        query_grad_tile = (
            jnp.einsum(
                "gqrmc,mcgd->rgqd", dscores_low, key_tile, preferred_element_type=jnp.float32
            )
            * scale_factor
        )
        key_part = (
            jnp.einsum(
                "gqrmc,rgqd->mcgd", dscores_low, query_tile, preferred_element_type=jnp.float32
            )
            * scale_factor
        )
        value_part = jnp.einsum(
            "gqrmc,rgqd->mcgd", probs_low, grad_tile, preferred_element_type=jnp.float32
        )
        update = jnp.concatenate(
            [key_part.reshape(count, BLK, half_width), value_part.reshape(count, BLK, half_width)],
            axis=-1,
        )
        return (query_grad_tile.reshape(BLK, -1), update)

    zeros_acc = jnp.zeros((slot_count, BLK, kv_width), jnp.float32)
    row_numbers = jnp.arange(qblocks, dtype=jnp.int32)
    entry_ids = jnp.arange(max_blocks, dtype=jnp.int32)
    live_all = entry_ids[None, :] < block_count[:, None]

    def one_block(accumulated, inputs):
        row_number, query_tile, grad_tile, out_tile, tile_index, tile_live, tile_position = inputs
        key_tile, value_tile = fetch_tiles(tile_position)
        masked = masked_scores(query_tile, key_tile, row_number, tile_index, tile_live)
        row_top, row_total = stats_of(masked)
        query_part, update = terms_from(
            masked, row_top, row_total, query_tile, grad_tile, out_tile, key_tile, value_tile
        )
        return (accumulated.at[tile_position].add(update), query_part.astype(jnp.bfloat16))

    inputs = (row_numbers, query_blocks, grad_blocks, out_blocks, block_index, live_all, position)
    accumulated, query_grad = lax.scan(one_block, zeros_acc, inputs)
    far_part = accumulated[qblocks + 3 :].reshape(seq_count, capacity, BLK, kv_width)
    returned = lax.all_to_all(far_part, "seq", split_axis=0, concat_axis=0, tiled=True)
    own_grad = accumulated[:qblocks]
    returned_prev = shifted(
        accumulated[qblocks : qblocks + 2].astype(jnp.bfloat16), "seq", -1
    ).astype(jnp.float32)
    own_grad = own_grad.at[qblocks - 2 :].add(returned_prev)
    selector = (
        asked_rows.reshape(-1)[None, :] == jnp.arange(qblocks, dtype=jnp.int32)[:, None]
    ).astype(jnp.float32)
    far_terms = returned.reshape(seq_count * capacity, BLK * kv_width)
    own_grad = own_grad + jnp.dot(selector, far_terms, precision=lax.Precision.HIGHEST).reshape(
        qblocks, BLK, kv_width
    )
    first_total = lax.psum(accumulated[qblocks + 2], "seq")
    own_grad = own_grad.at[0].add(
        jnp.where(my_index == 0, first_total, jnp.zeros_like(first_total))
    )
    key_grad = own_grad[..., :half_width].reshape(qblocks * BLK, half_width).astype(jnp.bfloat16)
    value_grad = own_grad[..., half_width:].reshape(qblocks * BLK, half_width).astype(jnp.bfloat16)
    return (query_grad.reshape(qblocks * BLK, -1), key_grad, value_grad)


def solution(mesh):
    return jax.shard_map(
        local,
        mesh=mesh,
        in_specs=(
            P("seq", "head"),
            P("seq", "head"),
            P("seq", "head"),
            P("seq", "head"),
            P(("seq", "head"), None),
            P("seq", None),
            P("seq"),
        ),
        out_specs=(P("seq", "head"), P("seq", "head"), P("seq", "head")),
        check_vma=False,
    )
```

profile of v0, /device:TPU:0, one launch (start us, length us, event | category | flops | bytes accessed | tf_op | source)
XLA Modules:
  0.0 647.8 jit_solution(7845131346142039962)
XLA Ops:
  11.5 7.3 %all-to-all-start = ((s32[8,1,4]{2,1,0:T(1,128)}), s32[8,1,4]{2,1,0:T(1,128)S(1)}, u32[]{:S(2)}, u32[]{:S(2)}) async-start(s32[8,1,4]{2,1,0:T(1,128)} %bitcast.5), calls=%async_computation | async-start | bytes 8192 | tf_op jit(solution)/shard_map/all_to_all | solution.py:77
  22.0 3.3 all-to-all-done
  25.2 3.6 all-to-all-start.2
  34.1 20.4 %all-to-all-done.2 = bf16[256,4,1024]{2,0,1:T(8,128)(2,1)S(1)} async-done(((bf16[256,4,1024]{2,0,1:T(8,128)(2,1)}), bf16[256,4,1024]{2,0,1:T(8,128)(2,1)S(1)}, u32[]{:S(2)}, u32[]{:S(2)}) %all-to-all-start.2) | async-done | bytes 2097184 | tf_op jit(solution)/shard_map/all_to_all | solution.py:67
  54.5 4.6 all-to-all-start.1
  59.8 3.8 collective-permute-start
  64.3 4.4 reshape.378
  68.7 4.5 reshape.379
  75.9 102.6 %all-reduce.3.cloned.1.call-done = bf16[1,128,512]{2,1,0:T(8,128)(2,1)} async-done(((bf16[1,128,512]{2,1,0:T(8,128)(2,1)}), bf16[1,128,512]{2,1,0:T(8,128)(2,1)}) %all-reduce.3.cloned.1.call-update) | async-done | bytes 131088 | tf_op jit(solution)/shard_map/psum | solution.py:20
  178.5 7.0 %pad_maximum_fusion.1 = bf16[43,128,512]{2,1,0:T(8,128)(2,1)} fusion(bf16[32,128,512]{2,1,0:T(8,128)(2,1)} %bitcast.8, bf16[1,128,512]{2,1,0:T(8,128)(2,1)} %all-reduce.3.cloned.1.call-done, bf16[2,128,512]{2,1,0:T(8,128)(2,1)S(1)} %collective-permute-done, bf16[8,128,512]{2,1,0:T(8,128)(2,1)S(1)} %bitcast.206), kind=kLoop, calls=%fused_computation.58 | loop fusion | flops 8454144 | bytes 11272192 | tf_op jit(solution)/shard_map/concatenate | solution.py:82
  185.5 5.6 broadcast_in_dim.31
  191.1 187.3 %while.18 = (s32[]{:T(128)}, f32[43,128,512]{2,1,0:T(8,128)}, bf16[8,128,1024]{2,1,0:T(8,128)(2,1)}, s32[8,8]{1,0:T(8,128)S(1)}, bf16[8,128,2,4,128]{4,3,2,1,0:T...) while((s32[]{:T(128)}, f32[43,128,512]{2,1,0:T(8,128)}, ...), condition=%wide.region_8.9_spmd.clone.clone, body=%wide.region_3.8_spmd.clone.clone.sunk | while | flops 1364458624 | bytes 57066980 | solution.py:165
  195.9 3.2 gather_fusion
  210.2 4.2 scatter_fusion
  219.2 3.2 gather_fusion
  233.6 4.4 scatter_fusion
  242.7 3.2 gather_fusion
  257.0 4.5 scatter_fusion
  266.3 3.2 gather_fusion
  280.6 4.5 scatter_fusion
  289.9 3.2 gather_fusion
  304.2 4.3 scatter_fusion
  313.3 3.2 gather_fusion
  327.6 4.1 scatter_fusion
  350.8 4.2 scatter_fusion
  374.1 4.4 scatter_fusion
  378.5 8.2 %slice.98 = f32[32,128,512]{2,1,0:T(8,128)} slice(f32[43,128,512]{2,1,0:T(8,128)} %get-tuple-element.181), slice={[11:43], [0:128], [0:512]} | slice | bytes 16777216 | tf_op jit(solution)/shard_map/slice | solution.py:166
  386.7 4.9 all-to-all-start.3
  397.0 15.4 %copy.156 = f32[43,128,512]{2,0,1:T(8,128)} copy(f32[43,128,512]{2,1,0:T(8,128)} %get-tuple-element.181) | data formatting | bytes 22544384 | tf_op jit(solution)/shard_map/while | solution.py:165
  412.4 201.8 %all-reduce.5.cloned.1.call-done = f32[128,512]{1,0:T(8,128)} async-done(((f32[128,512]{1,0:T(8,128)}), f32[128,512]{1,0:T(8,128)}) %all-reduce.5.cloned.1.call-update) | async-done | bytes 262160 | tf_op jit(solution)/shard_map/psum | solution.py:180
  616.9 12.4 %fusion.44 = f32[8,128,512]{2,0,1:T(8,128)S(1)} fusion(f32[8,128,512]{2,0,1:T(8,128)S(1)} %copy_dynamic-update-slice_fusion, s32[32]{0:T(128)S(1)} %eq.62, f32[4,8,128,512]{3,2,1,0:T(8,128)} %bitcast.70), kind=kOutput, calls=%fused_computation.60 | convolution fusion | flops 201851136 | bytes 12583040 | tf_op jit(solution)/shard_map/dot_general | solution.py:177
  631.1 6.3 scatter-add.20
  (263 shorter events, 157.4 us)
Async XLA Ops:
  11.5 13.7 %all-to-all-start = ((s32[8,1,4]{2,1,0:T(1,128)}), s32[8,1,4]{2,1,0:T(1,128)S(1)}, u32[]{:S(2)}, u32[]{:S(2)}) async-start(s32[8,1,4]{2,1,0:T(1,128)} %bitcast.5), calls=%async_computation | async-start | bytes 8192 | tf_op jit(solution)/shard_map/all_to_all | solution.py:77
  25.2 29.3 %all-to-all-start.2 = ((bf16[256,4,1024]{2,0,1:T(8,128)(2,1)}), bf16[256,4,1024]{2,0,1:T(8,128)(2,1)S(1)}, u32[]{:S(2)}, u32[]{:S(2)}) async-start(bf16[256,4,1024]{2,0,1:T(8,128)(2,1)} %bitcast.211), calls=%async_computation.2 | async-start | bytes 4194304 | tf_op jit(solution)/shard_map/all_to_all | solution.py:67
  54.5 124.0 %all-to-all-start.1 = ((bf16[8,4,128,512]{3,2,1,0:T(8,128)(2,1)}), bf16[8,4,128,512]{3,2,1,0:T(8,128)(2,1)}, u32[]{:S(2)}, u32[]{:S(2)}) async-start(bf16[8,4,128,512]{3,2,1,0:T(8,128)(2,1)} %bitcast.208), calls=%async_computation.1 | async-start | bytes 8388608 | tf_op jit(solution)/shard_map/all_to_all | solution.py:79
  59.1 119.5 %all-reduce.3.cloned.1.call-start = ((), (), s32[]{:S(2)}) async-start(), calls=%async_computation.4 | async-start | bytes 262144 | tf_op jit(solution)/shard_map/psum | solution.py:20
  59.8 118.7 %collective-permute-start = (bf16[2,128,512]{2,1,0:T(8,128)(2,1)}, bf16[2,128,512]{2,1,0:T(8,128)(2,1)S(1)}, u32[]{:S(2)}, u32[]{:S(2)}) collective-permute-start(bf16[2,128,512]{2,1,0:T(8,128)(2,1)} %bitcast.1), channel_id=1, source_target_pairs={{0,4},{4,8},{8,12},{12,16},{16,20},{20,24},{24,28},{1,5},{5,9},{9,... | collective-permute-start | bytes 786440 | tf_op jit(solution)/shard_map/ppermute | solution.py:15
  386.7 230.2 %all-to-all-start.3 = ((f32[8,4,128,512]{3,2,1,0:T(8,128)}), f32[8,4,128,512]{3,2,1,0:T(8,128)}, u32[]{:S(2)}, u32[]{:S(2)}) async-start(f32[8,4,128,512]{3,2,1,0:T(8,128)} %bitcast.207), calls=%async_computation.3 | async-start | bytes 16777216 | tf_op jit(solution)/shard_map/all_to_all | solution.py:167
  391.6 222.6 %all-reduce.5.cloned.1.call-start = ((), (), s32[]{:S(2)}) async-start(), calls=%async_computation.5 | async-start | bytes 524288 | tf_op jit(solution)/shard_map/psum | solution.py:180
  394.5 220.7 %collective-permute-start.1 = (bf16[2,128,512]{2,1,0:T(8,128)(2,1)S(1)}, bf16[2,128,512]{2,1,0:T(8,128)(2,1)S(1)}, u32[]{:S(2)}, u32[]{:S(2)}) collective-permute-start(bf16[2,128,512]{2,1,0:T(8,128)(2,1)S(1)} %slice.127), channel_id=1, source_target_pairs={{4,0},{8,4},{12,8},{16,12},{20,16},{24,20},{28,24},{5,1},{9,5},{13... | collective-permute-start | bytes 786440 | tf_op jit(solution)/shard_map/ppermute | solution.py:15
  412.4 203.9 %slice-start = ((f32[43,128,512]{2,0,1:T(8,128)}), f32[8,128,512]{2,0,1:T(8,128)S(1)}, s32[]{:S(2)}) async-start(f32[43,128,512]{2,0,1:T(8,128)} %copy.156), calls=%async_computation.6 | async-start | bytes 4194304 | tf_op jit(solution)/shard_map/slice | solution.py:168
  629.4 1.3 copy-start
Sparse Core Ops, SparseCore 0:
  64.4 114.0 all-reduce.2
  396.4 217.7 all-reduce.4
where the time goes:
time: 651 us; the launch traced here: 648 us
  waiting for transfers between devices  328 us (50%)
  local copies, waits for them, and re-layouts  143 us (22%)
  other arithmetic  78.1 us (12%)
  matrix products  53 us (8%)
  starting transfers between devices  25.5 us (4%)
  between operations  14.2 us (2%)
    psum x1, waiting for transfers between devices, local(): first_total = lax.psum(accumulated[qblocks + 2], 'seq')  202 us
    psum x1, waiting for transfers between devices, broadcast(): return lax.psum(jnp.where(mine, x, jnp.zeros_like(x)), axis)  103 us
    scatter-add x8, other arithmetic, one_block(): accumulated.at[tile_position].add(update)  34.5 us
    gather x8, local copies, waits for them, and re-layouts, fetch_tiles(): gathered = kv_all[tile_position]  25.7 us
    dynamic_slice x24, local copies, waits for them, and re-layouts, local(): accumulated, query_grad = lax.scan(one_block, zeros_acc, inputs)  22.8 us
    all_to_all x1, waiting for transfers between devices, local(): lax.all_to_all(out_grad, 'head', split_axis=1, concat_axis=0, tiled=True)  20.4 us
    while x1, local copies, waits for them, and re-layouts, local(): accumulated, query_grad = lax.scan(one_block, zeros_acc, inputs)  15.4 us
    concatenate x8, local copies, waits for them, and re-layouts, terms_from(): jnp.concatenate([key_part.reshape(count, BLK, half_width), value_part.res...  15.3 us
  transfers between devices with their start and end apart: 8, of which 4 were waited for; matrix products, arithmetic and copies ran while one was open for 7% of the time, Pallas kernels for 0%

commit v1 on v0

v1 whole, which is shorter than its diff:
```python
import functools

import jax
import jax.numpy as jnp
from jax import lax
from jax.experimental import pallas as pl
from jax.experimental.pallas import tpu as pltpu
from jax.sharding import PartitionSpec as P

HD = 128
GROUP = 4
BLK = 128
NF = 4
LOG2E = 1.4426950408889634


def shifted(value, axis, steps):
    count = lax.axis_size(axis)
    initial, last = (max(0, -steps), min(count, count - steps))
    return lax.ppermute(value, axis, [(source, source + steps) for source in range(initial, last)])


def spread_first(x, axis):
    count = lax.axis_size(axis)
    me = lax.axis_index(axis)
    step = 1
    while step < count:
        pairs = [(i, i + step) for i in range(step) if i + step < count]
        got = lax.ppermute(x, axis, pairs)
        x = jnp.where(me < step, x, got)
        step *= 2
    return x


def sum_to_first(x, axis):
    count = lax.axis_size(axis)
    step = 1
    while step < count:
        step *= 2
    step //= 2
    while step >= 1:
        pairs = [(i + step, i) for i in range(step) if i + step < count]
        x = x + lax.ppermute(x, axis, pairs)
        step //= 2
    return x


def live_far(block_index, block_count, device, qblocks):
    owner = block_index // qblocks
    within = block_index % qblocks
    max_blocks = block_index.shape[-1]
    live = jnp.arange(max_blocks, dtype=jnp.int32) < block_count[..., None]
    is_local = owner == device
    is_prev = (owner == device - 1) & (within >= qblocks - 2)
    is_first = (block_index == 0) & ~is_local & ~is_prev
    is_far = live & ~is_local & ~is_prev & ~is_first
    return owner, within, is_local, is_prev, is_first, is_far


def positions_of(block_index, block_count, device, qblocks, capacity):
    owner, within, is_local, is_prev, is_first, is_far = live_far(
        block_index, block_count, device, qblocks
    )
    flat_far = is_far.reshape(-1)
    flat_owner = owner.reshape(-1)
    order = jnp.arange(flat_far.shape[0], dtype=jnp.int32)
    earlier = (
        flat_far[None, :]
        & (flat_owner[None, :] == flat_owner[:, None])
        & (order[None, :] < order[:, None])
    )
    rank = jnp.sum(earlier.astype(jnp.int32), axis=1).reshape(block_index.shape)
    far_position = qblocks + 3 + owner * capacity + rank
    return jnp.where(
        is_local,
        within,
        jnp.where(is_prev, within + 2, jnp.where(is_first, qblocks + 2, far_position)),
    )


def asked_of(tables, counts, me, qblocks, capacity):
    devices = tables.shape[0]
    who = jnp.arange(devices, dtype=jnp.int32)[:, None, None]
    owner, within, _, _, _, is_far = live_far(tables, counts, who, qblocks)
    mine = (is_far & (owner == me)).reshape(devices, -1)
    order = jnp.arange(mine.shape[1], dtype=jnp.int32)
    earlier = mine[:, None, :] & (order[None, None, :] < order[None, :, None])
    rank = jnp.sum(earlier.astype(jnp.int32), axis=2)
    slots = jnp.arange(capacity, dtype=jnp.int32)
    chosen = mine[:, None, :] & (rank[:, None, :] == slots[None, :, None])
    blocks = jnp.where(chosen, within.reshape(devices, 1, -1), 0)
    return jnp.sum(blocks, axis=2).reshape(-1)


def serve_kernel(capacity, kv_heads, asked_ref, k_ref, v_ref, out_ref):
    base = pl.program_id(0) * capacity
    for c in range(capacity):
        start = pl.multiple_of(asked_ref[base + c] * BLK, BLK)
        for h in range(kv_heads):
            cols = slice(h * HD, (h + 1) * HD)
            rows = slice(c * BLK, (c + 1) * BLK)
            out_ref[rows, 2 * h * HD : (2 * h + 1) * HD] = k_ref[pl.ds(start, BLK), cols]
            out_ref[rows, (2 * h + 1) * HD : (2 * h + 2) * HD] = v_ref[pl.ds(start, BLK), cols]


def serve(asked, key_rows, value_rows, capacity):
    kv_heads = key_rows.shape[1] // HD
    width = 2 * kv_heads * HD
    devices = asked.shape[0] // capacity
    whole = pl.BlockSpec(key_rows.shape, lambda s, a: (0, 0))
    return pl.pallas_call(
        functools.partial(serve_kernel, capacity, kv_heads),
        grid_spec=pltpu.PrefetchScalarGridSpec(
            num_scalar_prefetch=1,
            grid=(devices,),
            in_specs=[whole, whole],
            out_specs=pl.BlockSpec((capacity * BLK, width), lambda s, a: (s, 0)),
        ),
        out_shape=jax.ShapeDtypeStruct((devices * capacity * BLK, width), key_rows.dtype),
        cost_estimate=pl.CostEstimate(flops=0, bytes_accessed=6 << 20, transcendentals=0),
        name="serve",
    )(asked, key_rows, value_rows)


def attend_kernel(
    qblocks, entries, pos_ref, cnt_ref, q_ref, g_ref, o_ref, k_ref, v_ref, near_ref, far_ref,
    dq_ref, own_ref, dnear_ref, dfar_ref, kv_ref, acc_ref,
):
    r = pl.program_id(1)
    near_top = qblocks + 3

    @pl.when(r == 0)
    def _():
        own_ref[...] = jnp.zeros_like(own_ref)
        dnear_ref[...] = jnp.zeros_like(dnear_ref)
        acc_ref[...] = jnp.zeros_like(acc_ref)

    def at(slot):
        return pl.ds(pl.multiple_of(slot * BLK, BLK), BLK)

    for e in range(entries):
        p = pos_ref[r * entries + e]
        rows = slice(e * BLK, (e + 1) * BLK)

        @pl.when(p < qblocks)
        def _():
            kv_ref[rows, :HD] = k_ref[at(p), :]
            kv_ref[rows, HD:] = v_ref[at(p), :]

        @pl.when((p >= qblocks) & (p < near_top))
        def _():
            kv_ref[rows, :] = near_ref[at(p - qblocks), :]

        @pl.when(p >= near_top)
        def _():
            kv_ref[rows, :] = far_ref[at(p - near_top), :]

    def stacked(ref):
        return jnp.concatenate([ref[:, g * HD : (g + 1) * HD] for g in range(GROUP)], axis=0)

    scale = HD ** (-0.5)
    q = stacked(q_ref)
    g = stacked(g_ref)
    keys = kv_ref[:, :HD]
    values = kv_ref[:, HD:]
    contract_last = (((1,), (1,)), ((), ()))
    scores = lax.dot_general(keys, q, contract_last, preferred_element_type=jnp.float32)
    count = cnt_ref[r]
    shape = (BLK, GROUP * BLK)
    causal = lax.broadcasted_iota(jnp.int32, shape, 0) <= (
        lax.broadcasted_iota(jnp.int32, shape, 1) % BLK
    )
    parts = [jnp.where(causal, scores[:BLK], -jnp.inf)]
    for e in range(1, entries):
        bias = jnp.where(e < count, 0.0, -jnp.inf).astype(jnp.float32)
        parts.append(scores[e * BLK : (e + 1) * BLK] + bias)
    masked = jnp.concatenate(parts, axis=0)
    top = jnp.max(masked, axis=0, keepdims=True)
    powers = jnp.exp2((masked - top) * (scale * LOG2E))
    total = jnp.sum(powers, axis=0, keepdims=True)
    probs = powers * (1.0 / total)
    probs_low = probs.astype(jnp.bfloat16)
    out_prod = g.astype(jnp.float32) * stacked(o_ref).astype(jnp.float32)
    out_dot = jnp.sum(jnp.transpose(out_prod), axis=0, keepdims=True)
    dprobs = lax.dot_general(values, g, contract_last, preferred_element_type=jnp.float32)
    dscores = (probs * (dprobs - out_dot)).astype(jnp.bfloat16)
    dq = jnp.dot(jnp.transpose(keys), dscores, preferred_element_type=jnp.float32) * scale
    dq = jnp.transpose(dq).astype(dq_ref.dtype)
    for i in range(GROUP):
        dq_ref[:, i * HD : (i + 1) * HD] = dq[i * BLK : (i + 1) * BLK]
    dkeys = jnp.dot(dscores, q, preferred_element_type=jnp.float32) * scale
    dvalues = jnp.dot(probs_low, g, preferred_element_type=jnp.float32)

    for e in range(entries):
        p = pos_ref[r * entries + e]
        dk = dkeys[e * BLK : (e + 1) * BLK]
        dv = dvalues[e * BLK : (e + 1) * BLK]

        def add(ref, slot, dk=dk, dv=dv):
            ref[at(slot), :HD] += dk
            ref[at(slot), HD:] += dv

        @pl.when(p < qblocks)
        def _():
            add(own_ref, p)

        @pl.when((p >= qblocks) & (p < near_top))
        def _():
            add(dnear_ref, p - qblocks)

        @pl.when(p >= near_top)
        def _():
            add(acc_ref, p - near_top)

    @pl.when(r == qblocks - 1)
    def _():
        dfar_ref[...] = acc_ref[...].astype(dfar_ref.dtype)


def attend(position, count, query_rows, grad_rows, attn_out, key_rows, value_rows, near, far):
    qblocks, entries = position.shape
    kv_heads = key_rows.shape[1] // HD
    rows = query_rows.shape[0]
    wide = GROUP * HD
    by_row = pl.BlockSpec((BLK, wide), lambda h, r, *_: (r, h))

    def by_head(height, width):
        return pl.BlockSpec((height, width), lambda h, r, *_: (0, h))

    f32 = jnp.float32
    pairs = qblocks * entries * kv_heads * GROUP
    return pl.pallas_call(
        functools.partial(attend_kernel, qblocks, entries),
        grid_spec=pltpu.PrefetchScalarGridSpec(
            num_scalar_prefetch=2,
            grid=(kv_heads, qblocks),
            in_specs=[
                by_row, by_row, by_row,
                by_head(rows, HD), by_head(rows, HD),
                by_head(near.shape[0], 2 * HD), by_head(far.shape[0], 2 * HD),
            ],
            out_specs=[
                by_row, by_head(rows, 2 * HD), by_head(near.shape[0], 2 * HD),
                by_head(far.shape[0], 2 * HD),
            ],
            scratch_shapes=[
                pltpu.VMEM((entries * BLK, 2 * HD), key_rows.dtype),
                pltpu.VMEM((far.shape[0], 2 * HD), f32),
            ],
        ),
        out_shape=[
            jax.ShapeDtypeStruct(query_rows.shape, query_rows.dtype),
            jax.ShapeDtypeStruct((rows, 2 * kv_heads * HD), f32),
            jax.ShapeDtypeStruct(near.shape, f32),
            jax.ShapeDtypeStruct(far.shape, far.dtype),
        ],
        compiler_params=pltpu.CompilerParams(
            dimension_semantics=("arbitrary", "arbitrary"), vmem_limit_bytes=56 << 20
        ),
        cost_estimate=pl.CostEstimate(
            flops=pairs * 10 * BLK * BLK * HD,
            bytes_accessed=24 << 20,
            transcendentals=pairs * BLK * BLK,
        ),
        name="attend",
    )(
        position.reshape(-1), count, query_rows, grad_rows, attn_out, key_rows, value_rows,
        near, far,
    )


def finish_kernel(qblocks, slots, asked_ref, own_ref, back_ref, prev_ref, first_ref,
                  dk_ref, dv_ref, acc_ref):
    acc_ref[...] = own_ref[...]
    acc_ref[:BLK] += first_ref[...]
    acc_ref[(qblocks - 2) * BLK :] += prev_ref[...].astype(jnp.float32)
    for s in range(slots):
        rows = pl.ds(pl.multiple_of(asked_ref[s] * BLK, BLK), BLK)
        acc_ref[rows, :] += back_ref[s * BLK : (s + 1) * BLK, :].astype(jnp.float32)
    dk_ref[...] = acc_ref[:, :HD].astype(dk_ref.dtype)
    dv_ref[...] = acc_ref[:, HD:].astype(dv_ref.dtype)


def finish(asked, own, back, prev, first, dtype):
    rows, width = own.shape
    kv_heads = width // (2 * HD)

    def by_head(height, columns):
        return pl.BlockSpec((height, columns), lambda h, a: (0, h))

    out = jax.ShapeDtypeStruct((rows, kv_heads * HD), dtype)
    return pl.pallas_call(
        functools.partial(finish_kernel, rows // BLK, asked.shape[0]),
        grid_spec=pltpu.PrefetchScalarGridSpec(
            num_scalar_prefetch=1,
            grid=(kv_heads,),
            in_specs=[by_head(x.shape[0], 2 * HD) for x in (own, back, prev, first)],
            out_specs=[by_head(rows, HD), by_head(rows, HD)],
            scratch_shapes=[pltpu.VMEM((rows, 2 * HD), jnp.float32)],
        ),
        out_shape=[out, out],
        cost_estimate=pl.CostEstimate(flops=0, bytes_accessed=8 << 20, transcendentals=0),
        name="finish",
    )(asked, own, back, prev, first)


def interleave(key_rows, value_rows):
    heads = key_rows.shape[1] // HD
    parts = []
    for h in range(heads):
        cols = slice(h * HD, (h + 1) * HD)
        parts += [key_rows[:, cols], value_rows[:, cols]]
    return jnp.concatenate(parts, axis=1)


def local(query_rows, key_rows, value_rows, attn_out, out_grad, block_index, block_count):
    seq_count = lax.axis_size("seq")
    me = lax.axis_index("seq")
    qblocks = query_rows.shape[0] // BLK
    capacity = qblocks * NF // seq_count
    width = 2 * key_rows.shape[1]
    tables = lax.all_gather(
        jnp.concatenate([block_index, block_count[:, None]], axis=1), "seq", axis=0
    )
    asked = asked_of(tables[..., :-1], tables[..., -1], me, qblocks, capacity)
    position = positions_of(block_index, block_count, me, qblocks, capacity)
    grad_rows = lax.all_to_all(out_grad, "head", split_axis=1, concat_axis=0, tiled=True)
    served = serve(asked, key_rows, value_rows, capacity)
    far = lax.all_to_all(served, "seq", split_axis=0, concat_axis=0, tiled=True)
    tail = interleave(key_rows[(qblocks - 2) * BLK :], value_rows[(qblocks - 2) * BLK :])
    head = interleave(key_rows[:BLK], value_rows[:BLK])
    near = jnp.concatenate([shifted(tail, "seq", 1), spread_first(head, "seq")], axis=0)
    query_grad, own, dnear, dfar = attend(
        position, block_count, query_rows, grad_rows, attn_out, key_rows, value_rows, near, far
    )
    back = lax.all_to_all(dfar, "seq", split_axis=0, concat_axis=0, tiled=True)
    prev = shifted(dnear[: 2 * BLK].astype(jnp.bfloat16), "seq", -1)
    mine = dnear[2 * BLK :]
    first = sum_to_first(mine, "seq")
    first = jnp.where(me == 0, first, jnp.zeros_like(first))
    key_grad, value_grad = finish(asked, own, back, prev, first, key_rows.dtype)
    return (query_grad, key_grad, value_grad)


def solution(mesh):
    return jax.shard_map(
        local,
        mesh=mesh,
        in_specs=(
            P("seq", "head"),
            P("seq", "head"),
            P("seq", "head"),
            P("seq", "head"),
            P(("seq", "head"), None),
            P("seq", None),
            P("seq"),
        ),
        out_specs=(P("seq", "head"), P("seq", "head"), P("seq", "head")),
        check_vma=False,
    )
```

time: 651 us -> 337 us (0.52)
  local copies, waits for them, and re-layouts: 143 us -> 9.24 us
  waiting for transfers between devices: 328 us -> 197 us
  other arithmetic: 78.1 us -> 2.58 us
  Pallas kernels: 0 us -> 56.8 us
  matrix products: 53 us -> 0 us
  blocking collectives: 0 us -> 31.8 us
  between operations: 14.2 us -> 0.84 us
  starting transfers between devices: 25.5 us -> 37.9 us
    psum x2 -> x0, waiting for transfers between devices: 304 us -> none  [the longest x1 202 us: local(): first_total = lax.psum(accumulated[qblocks + 2], 'seq')]
    ppermute x0 -> x6, waiting for transfers between devices: none -> 178 us  [the longest x3 119 us: sum_to_first(): x = x + lax.ppermute(x, axis, pairs)]
    pallas_call x0 -> x3, Pallas kernels: none -> 56.8 us  [the longest x1 46.3 us: attend(): pl.pallas_call(functools.partial(attend_kernel, qblocks, entries), grid_s...]
    dot_general x41 -> x0, matrix products: 53 us -> none  [the longest x8 13 us: terms_from(): jnp.einsum('rgqd,mcgd->gqrmc', grad_tile, value_tile, preferred_element_t...]
    scatter-add x8 -> x0, other arithmetic: 34.5 us -> none  [one_block(): accumulated.at[tile_position].add(update)]
    all_gather x0 -> x1, blocking collectives: none -> 31.8 us  [local(): lax.all_gather(jnp.concatenate([block_index, block_count[:, None]], axis=...]
    gather x9 -> x0, local copies, waits for them, and re-layouts: 28.4 us -> none  [the longest x8 25.7 us: fetch_tiles(): gathered = kv_all[tile_position]]
    dynamic_slice x24 -> x0, local copies, waits for them, and re-layouts: 22.8 us -> none  [local(): accumulated, query_grad = lax.scan(one_block, zeros_acc, inputs)]
  transfers between devices with their start and end apart: 8 -> 11, of which waited for: 4 -> 8; matrix products, arithmetic and copies ran while one was open for 7% -> 2% of each run, Pallas kernels for 0% -> 2%
where the time goes in v1:
time: 337 us
  waiting for transfers between devices  197 us (58%)
  Pallas kernels  56.8 us (17%)
  starting transfers between devices  37.9 us (11%)
  blocking collectives  31.8 us (9%)
  local copies, waits for them, and re-layouts  9.24 us (3%)
    ppermute x3, waiting for transfers between devices, sum_to_first(): x = x + lax.ppermute(x, axis, pairs)  119 us
    ppermute x3, waiting for transfers between devices, spread_first(): got = lax.ppermute(x, axis, pairs)  59.2 us
    pallas_call x1, Pallas kernels, attend(): pl.pallas_call(functools.partial(attend_kernel, qblocks, entries), grid_s...  46.3 us
    all_gather x1, blocking collectives, local(): lax.all_gather(jnp.concatenate([block_index, block_count[:, None]], axis=...  31.8 us
    all_to_all x1, waiting for transfers between devices, local(): far = lax.all_to_all(served, 'seq', split_axis=0, concat_axis=0, tiled=True)  16.8 us
    all_to_all x1, starting transfers between devices, local(): back = lax.all_to_all(dfar, 'seq', split_axis=0, concat_axis=0, tiled=True)  15 us
  transfers between devices with their start and end apart: 11, of which 8 were waited for; matrix products, arithmetic and copies ran while one was open for 2% of the time, Pallas kernels for 2%

profile of v1, /device:TPU:0, one launch (start us, length us, event | category | flops | bytes accessed | tf_op | source)
XLA Modules:
  0.0 336.5 jit_solution(9862115371033346464)
XLA Ops:
  0.6 3.1 copy.29
  3.8 4.4 %all-to-all-start = ((bf16[256,4,1024]{2,0,1:T(8,128)(2,1)}), bf16[256,4,1024]{2,0,1:T(8,128)(2,1)S(1)}, u32[]{:S(2)}, u32[]{:S(2)}) async-start(bf16[256,4,1024]{2,0,1:T(8,128)(2,1)} %bitcast.13), calls=%async_computation | async-start | bytes 4194304 | tf_op jit(solution)/shard_map/all_to_all | solution.py:327
  8.3 31.8 %all-gather = s32[64,9]{1,0:T(8,128)S(1)} all-gather(s32[8,9]{1,0:T(8,128)S(1)} %pad_add_fusion), channel_id=2, replica_groups=mesh['seq'=8,'head'=4] {'seq'}, dimensions={0}, use_global_device_ids=true | all-gather | bytes 2592 | tf_op jit(solution)/shard_map/all_gather | solution.py:322
  41.3 0.6 reshape.52.asked_ref
  41.9 5.7 %serve.1 = bf16[4096,512]{1,0:T(8,128)(2,1)} custom-call(s32[32]{0:T(128)} %reshape.52.asked_ref, bf16[1024,256]{1,0:T(8,128)(2,1)} %k_ref.3, bf16[1024,256]{1,0:T(8,128)(2,1)} %v_ref.3), custom_call_target="tpu_custom_call" | custom-call | bytes 6291456 | tf_op jit(solution)/shard_map/serve/pallas_call | solution.py:111
  47.6 1.3 copy-done
  48.9 5.5 %all-to-all-start.1 = ((bf16[8,512,512]{2,1,0:T(8,128)(2,1)}), bf16[8,512,512]{2,1,0:T(8,128)(2,1)}, u32[]{:S(2)}, u32[]{:S(2)}) async-start(bf16[8,512,512]{2,1,0:T(8,128)(2,1)} %bitcast.15), calls=%async_computation.1 | async-start | bytes 8388608 | tf_op jit(solution)/shard_map/all_to_all | solution.py:329
  54.4 0.8 fusion.16
  55.3 3.9 %collective-permute-start.1 = (bf16[128,512]{1,0:T(8,128)(2,1)S(1)}, bf16[128,512]{1,0:T(8,128)(2,1)S(1)}, u32[]{:S(2)}, u32[]{:S(2)}) collective-permute-start(bf16[128,512]{1,0:T(8,128)(2,1)S(1)} %pad_maximum_fusion.2), channel_id=1, source_target_pairs={{0,4},{1,5},{2,6},{3,7}} | collective-permute-start | bytes 393224 | tf_op jit(solution)/shard_map/ppermute | solution.py:29
  59.2 1.0 fusion.14
  60.2 1.3 collective-permute-start
  61.5 27.8 %collective-permute-done.1 = bf16[128,512]{1,0:T(8,128)(2,1)S(1)} collective-permute-done((bf16[128,512]{1,0:T(8,128)(2,1)S(1)}, bf16[128,512]{1,0:T(8,128)(2,1)S(1)}, u32[]{:S(2)}, u32[]{:S(2)}) %collective-permute-start.1) | collective-permute-done | bytes 131104 | tf_op jit(solution)/shard_map/ppermute | solution.py:29
  89.4 1.3 collective-permute-start.2
  91.2 29.5 %collective-permute-done.2 = bf16[128,512]{1,0:T(8,128)(2,1)S(1)} collective-permute-done((bf16[128,512]{1,0:T(8,128)(2,1)S(1)}, bf16[128,512]{1,0:T(8,128)(2,1)S(1)}, u32[]{:S(2)}, u32[]{:S(2)}) %collective-permute-start.2) | collective-permute-done | bytes 131104 | tf_op jit(solution)/shard_map/ppermute | solution.py:29
  120.7 1.3 collective-permute-start.3
  122.1 0.6 reshape.51.pos_ref
  122.7 1.9 collective-permute-done.3
  124.6 0.8 pad_maximum_fusion.near_ref
  125.3 16.8 %all-to-all-done.1 = bf16[8,512,512]{2,1,0:T(8,128)(2,1)} async-done(((bf16[8,512,512]{2,1,0:T(8,128)(2,1)}), bf16[8,512,512]{2,1,0:T(8,128)(2,1)}, u32[]{:S(2)}, u32[]{:S(2)}) %all-to-all-start.1) | async-done | bytes 4194336 | tf_op jit(solution)/shard_map/all_to_all | solution.py:329
  142.2 46.3 %attend.1 = (bf16[1024,1024]{1,0:T(8,128)(2,1)}, f32[1024,512]{1,0:T(8,128)}, f32[384,512]{1,0:T(8,128)}, bf16[4096,512]{1,0:T(8,128)(2,1)}) custom-call(s32[64]{0:T(128)} %reshape.51.pos_ref, s32[8]{0:T(128)} %cnt_ref.1, bf16[1024,1024]{1,0:T(8,128)(2,1)} %q_ref.1, bf16[1024,1024]{1,0:T(8,128)(2,1)} %bitcast.18, bf16[1024,1024]{1,0:T(8,128)(2,1)} %o_ref.1, ...), custom_call_target="tpu_custom_call" | custom-call | flops 10737418240 | bytes 25165824 | tf_op jit(solution)/shard_map/attend/pallas_call | solution.py:232
  188.5 15.0 %all-to-all-start.2 = ((bf16[8,512,512]{2,1,0:T(8,128)(2,1)}), bf16[8,512,512]{2,1,0:T(8,128)(2,1)}, u32[]{:S(2)}, u32[]{:S(2)}) async-start(bf16[8,512,512]{2,1,0:T(8,128)(2,1)} %bitcast.16), calls=%async_computation.2 | async-start | bytes 8388608 | tf_op jit(solution)/shard_map/all_to_all | solution.py:336
  203.5 1.3 collective-permute-start.5
  204.8 103.3 %collective-permute-done.5 = f32[128,512]{1,0:T(8,128)S(1)} collective-permute-done((f32[128,512]{1,0:T(8,128)S(1)}, f32[128,512]{1,0:T(8,128)S(1)}, u32[]{:S(2)}, u32[]{:S(2)}) %collective-permute-start.5) | collective-permute-done | bytes 262176 | tf_op jit(solution)/shard_map/ppermute | solution.py:43
  308.1 1.3 collective-permute-start.6
  309.4 7.7 %collective-permute-done.6 = f32[128,512]{1,0:T(8,128)S(1)} collective-permute-done((f32[128,512]{1,0:T(8,128)S(1)}, f32[128,512]{1,0:T(8,128)S(1)}, u32[]{:S(2)}, u32[]{:S(2)}) %collective-permute-start.6) | collective-permute-done | bytes 262176 | tf_op jit(solution)/shard_map/ppermute | solution.py:43
  317.2 1.3 collective-permute-start.7
  318.5 1.3 collective-permute-start.4
  319.8 8.3 %collective-permute-done.7 = f32[128,512]{1,0:T(8,128)S(1)} collective-permute-done((f32[128,512]{1,0:T(8,128)S(1)}, f32[128,512]{1,0:T(8,128)S(1)}, u32[]{:S(2)}, u32[]{:S(2)}) %collective-permute-start.7) | collective-permute-done | bytes 262176 | tf_op jit(solution)/shard_map/ppermute | solution.py:43
  328.1 0.8 add_select_fusion.first_ref
  328.9 2.1 collective-permute-done.4.prev_ref
  331.0 0.7 copy-done.2
  331.7 4.8 %finish.1 = (bf16[1024,256]{1,0:T(8,128)(2,1)}, bf16[1024,256]{1,0:T(8,128)(2,1)}) custom-call(s32[32]{0:T(128)} %reshape.52.asked_ref, f32[1024,512]{1,0:T(8,128)} %get-tuple-element.10.own_ref, bf16[4096,512]{1,0:T(8,128)(2,1)} %bitcast.8.back_ref, bf16[256,512]{1,0:T(8,128)(2,1)} %copy-done.2, f32[128,512]{1,0:T(8,128)} %add_select_fusion.first_ref), custom_call_target="tpu_custom_call" | custom-call | bytes 8388608 | tf_op jit(solution)/shard_map/finish/pallas_call | solution.py:292
  (43 shorter events, 2.2 us)
Async XLA Ops:
  3.8 4.4 %copy-start.4 = (s32[8]{0:T(128)S(1)}, s32[8]{0:T(128)}, u32[]{:S(2)}) copy-start(s32[8]{0:T(128)} %cnt_ref.1) | copy-start | bytes 100
  3.8 4.5 %copy-start.3 = (s32[8,8]{1,0:T(8,128)S(1)}, s32[8,8]{1,0:T(8,128)}, u32[]{:S(2)}) copy-start(s32[8,8]{1,0:T(8,128)} %param.12) | copy-start | bytes 772
  3.8 43.8 %all-to-all-start = ((bf16[256,4,1024]{2,0,1:T(8,128)(2,1)}), bf16[256,4,1024]{2,0,1:T(8,128)(2,1)S(1)}, u32[]{:S(2)}, u32[]{:S(2)}) async-start(bf16[256,4,1024]{2,0,1:T(8,128)(2,1)} %bitcast.13), calls=%async_computation | async-start | bytes 4194304 | tf_op jit(solution)/shard_map/all_to_all | solution.py:327
  47.6 1.3 copy-start
  48.9 93.3 %all-to-all-start.1 = ((bf16[8,512,512]{2,1,0:T(8,128)(2,1)}), bf16[8,512,512]{2,1,0:T(8,128)(2,1)}, u32[]{:S(2)}, u32[]{:S(2)}) async-start(bf16[8,512,512]{2,1,0:T(8,128)(2,1)} %bitcast.15), calls=%async_computation.1 | async-start | bytes 8388608 | tf_op jit(solution)/shard_map/all_to_all | solution.py:329
  55.3 34.1 %collective-permute-start.1 = (bf16[128,512]{1,0:T(8,128)(2,1)S(1)}, bf16[128,512]{1,0:T(8,128)(2,1)S(1)}, u32[]{:S(2)}, u32[]{:S(2)}) collective-permute-start(bf16[128,512]{1,0:T(8,128)(2,1)S(1)} %pad_maximum_fusion.2), channel_id=1, source_target_pairs={{0,4},{1,5},{2,6},{3,7}} | collective-permute-start | bytes 393224 | tf_op jit(solution)/shard_map/ppermute | solution.py:29
  60.2 64.4 %collective-permute-start = (bf16[256,512]{1,0:T(8,128)(2,1)S(1)}, bf16[256,512]{1,0:T(8,128)(2,1)S(1)}, u32[]{:S(2)}, u32[]{:S(2)}) collective-permute-start(bf16[256,512]{1,0:T(8,128)(2,1)S(1)} %pad_maximum_fusion.1), channel_id=1, source_target_pairs={{0,4},{4,8},{8,12},{12,16},{16,20},{20,24},{24,28},{1,5},{5,9},{9,... | collective-permute-start | bytes 786440 | tf_op jit(solution)/shard_map/ppermute | solution.py:20
  89.4 31.3 %collective-permute-start.2 = (bf16[128,512]{1,0:T(8,128)(2,1)S(1)}, bf16[128,512]{1,0:T(8,128)(2,1)S(1)}, u32[]{:S(2)}, u32[]{:S(2)}) collective-permute-start(bf16[128,512]{1,0:T(8,128)(2,1)S(1)} %broadcast_select_fusion), channel_id=1, source_target_pairs={{0,8},{4,12},{1,9},{5,13},{2,10},{6,14},{3,11},{7,15}} | collective-permute-start | bytes 393224 | tf_op jit(solution)/shard_map/ppermute | solution.py:29
  120.7 3.8 %collective-permute-start.3 = (bf16[128,512]{1,0:T(8,128)(2,1)S(1)}, bf16[128,512]{1,0:T(8,128)(2,1)S(1)}, u32[]{:S(2)}, u32[]{:S(2)}) collective-permute-start(bf16[128,512]{1,0:T(8,128)(2,1)S(1)} %broadcast_select_fusion.1), channel_id=1, source_target_pairs={{0,16},{4,20},{8,24},{12,28},{1,17},{5,21},{9,25},{13,29},{2,18},{... | collective-permute-start | bytes 393224 | tf_op jit(solution)/shard_map/ppermute | solution.py:29
  188.5 15.0 %copy-start.1 = (f32[384,512]{1,0:T(8,128)S(1)}, f32[384,512]{1,0:T(8,128)}, u32[]{:S(2)}) copy-start(f32[384,512]{1,0:T(8,128)} %get-tuple-element.12) | copy-start | bytes 2359300
  188.5 142.5 %all-to-all-start.2 = ((bf16[8,512,512]{2,1,0:T(8,128)(2,1)}), bf16[8,512,512]{2,1,0:T(8,128)(2,1)}, u32[]{:S(2)}, u32[]{:S(2)}) async-start(bf16[8,512,512]{2,1,0:T(8,128)(2,1)} %bitcast.16), calls=%async_computation.2 | async-start | bytes 8388608 | tf_op jit(solution)/shard_map/all_to_all | solution.py:336
  203.5 104.6 %collective-permute-start.5 = (f32[128,512]{1,0:T(8,128)S(1)}, f32[128,512]{1,0:T(8,128)S(1)}, u32[]{:S(2)}, u32[]{:S(2)}) collective-permute-start(f32[128,512]{1,0:T(8,128)S(1)} %slice.60), channel_id=1, source_target_pairs={{16,0},{20,4},{24,8},{28,12},{17,1},{21,5},{25,9},{29,13},{18,2},{... | collective-permute-start | bytes 786440 | tf_op jit(solution)/shard_map/ppermute | solution.py:43
  308.1 9.0 %collective-permute-start.6 = (f32[128,512]{1,0:T(8,128)S(1)}, f32[128,512]{1,0:T(8,128)S(1)}, u32[]{:S(2)}, u32[]{:S(2)}) collective-permute-start(f32[128,512]{1,0:T(8,128)S(1)} %slice_add_fusion), channel_id=1, source_target_pairs={{8,0},{12,4},{9,1},{13,5},{10,2},{14,6},{11,3},{15,7}} | collective-permute-start | bytes 786440 | tf_op jit(solution)/shard_map/ppermute | solution.py:43
  317.2 11.0 %collective-permute-start.7 = (f32[128,512]{1,0:T(8,128)S(1)}, f32[128,512]{1,0:T(8,128)S(1)}, u32[]{:S(2)}, u32[]{:S(2)}) collective-permute-start(f32[128,512]{1,0:T(8,128)S(1)} %add.53), channel_id=1, source_target_pairs={{4,0},{5,1},{6,2},{7,3}} | collective-permute-start | bytes 786440 | tf_op jit(solution)/shard_map/ppermute | solution.py:43
  318.5 12.4 %collective-permute-start.4 = (bf16[256,512]{1,0:T(8,128)(2,1)S(1)}, bf16[256,512]{1,0:T(8,128)(2,1)S(1)}, u32[]{:S(2)}, u32[]{:S(2)}) collective-permute-start(bf16[256,512]{1,0:T(8,128)(2,1)S(1)} %slice.66), channel_id=1, source_target_pairs={{4,0},{8,4},{12,8},{16,12},{20,16},{24,20},{28,24},{5,1},{9,5},{13... | collective-permute-start | bytes 786440 | tf_op jit(solution)/shard_map/ppermute | solution.py:20
  331.0 0.7 copy-start.2
